TPU v7x, 32 devices: a whole 2x2x4 slice. The times are simulated.
32 devices in a mesh: row: 16 (over z, y, x), col: 2 (over core).
Axes of the slice: x: 2, y: 2, z: 4, core: 2. Of those that a mesh axis runs over, the one named last changes fastest.
Arguments:
- lanczos_now: float32 [1, 256, 1024], P(None, 'row', 'col'), may hold values from -80 to 80, as said below
- lanczos_prev: float32 [1, 256, 1024], P(None, 'row', 'col'), may hold values from -6 to 6
- beta_prev: float32 [1], replicated, may hold values from 0.3 to 1.5
- valence_energy: float32 [256], P('row'), may hold values from -1.5 to -0.5
- conduction_energy: float32 [1024], P('col'), may hold values from 0.5 to 2.5
- valence_panel: float32 [16384, 256], P(('row', 'col')), may hold values from -0.375 to 0.375
- conduction_panel: float32 [16384, 1024], P(('row', 'col')), may hold values from -0.1875 to 0.1875
- screened_coulomb: float32 [16384, 16384], P('row', 'col'), may hold values from -0.046875 to 0.046875
- bare_coulomb: float32 [16384, 16384], P('row', 'col'), may hold values from -0.046875 to 0.046875
Outputs:
- lanczos_next: float32 [1, 256, 1024], P(None, 'row', 'col')
- coefficients: float32 [1, 2], replicated
Inputs may be any that keep to these rules, and one draw needn't show every extreme that they name: `lanczos_now`: real entries; the vectors of a chain are not normalized.
All inputs are finite; a program needn't handle non-finite values.
Results may differ from a plain program's by a relative error of at most 0.0002.
Values sent between devices are 32-bit elements; how exact they have to be, the bound alone decides.
A program may use at most 192 MiB of HBM per device.

v0:
```python
import jax
import jax.numpy as jnp
from jax import lax
from jax.sharding import PartitionSpec as P

V = 256
C = 1024


precise = lax.Precision.HIGHEST
epsilon = 1e-06


def per_device(
    lanczos_now,
    lanczos_prev,
    beta_prev,
    valence_energy,
    conduction_energy,
    valence_panel,
    conduction_panel,
    screened_coulomb,
    bare_coulomb,
):
    column_points = screened_coulomb.shape[1]
    wider = lax.all_gather(lanczos_now, "col", axis=2, tiled=True)
    vectors = lax.all_gather(wider, "row", axis=1, tiled=True)
    products = jnp.einsum("pv,kvc->pkc", valence_panel, vectors, precision=precise)
    density = jnp.sum(products * conduction_panel[:, None, :], axis=2)
    pair_local = jnp.einsum("pc,kvc->pkv", conduction_panel, vectors, precision=precise)
    every_panel, every_density = (
        lax.all_gather(valence_panel, ("row", "col"), axis=0, tiled=True),
        lax.all_gather(density, ("row", "col"), axis=0, tiled=True),
    )
    first_point = lax.axis_index("col") * column_points
    panel = lax.dynamic_slice_in_dim(every_panel, first_point, column_points, 0)
    far_density = lax.dynamic_slice_in_dim(every_density, first_point, column_points, 0)
    pair_terms = (
        jnp.einsum(
            "mkv,nv->mkn",
            lax.all_gather(pair_local, "col", axis=0, tiled=True),
            panel,
            precision=precise,
        )
        * screened_coulomb[:, None, :]
    )
    screened = jnp.einsum("mkn,nv->mkv", pair_terms, panel, precision=precise)
    potential = jnp.dot(bare_coulomb, far_density, precision=precise)
    direct_rows, local_potential = (
        lax.psum_scatter(screened, "col", scatter_dimension=0, tiled=True),
        lax.psum_scatter(potential, "col", scatter_dimension=0, tiled=True),
    )
    weighted = local_potential[:, :, None] * conduction_panel[:, None, :]
    bare_term = jnp.einsum("pv,pkc->vkc", valence_panel, weighted, precision=precise)
    screened_term = jnp.einsum("mkv,mc->vkc", direct_rows, conduction_panel, precision=precise)
    band_rows = lax.psum_scatter(
        2.0 * bare_term - screened_term, "row", scatter_dimension=0, tiled=True
    )
    kernel_part = lax.psum_scatter(band_rows, "col", scatter_dimension=2, tiled=True)
    kernel_part = jnp.transpose(kernel_part, (1, 0, 2))
    gaps = conduction_energy[None, None, :] - valence_energy[None, :, None]
    image = gaps * lanczos_now + kernel_part
    inverse_size = 1.0 / (V * C)
    sum_qu, sum_qq = lax.psum(
        (
            jnp.sum(lanczos_now * image, axis=(1, 2)),
            jnp.sum(lanczos_now * lanczos_now, axis=(1, 2)),
        ),
        ("row", "col"),
    )
    coef_alpha = sum_qu * inverse_size / (sum_qq * inverse_size + epsilon)
    resid = (
        image - coef_alpha[:, None, None] * lanczos_now - beta_prev[:, None, None] * lanczos_prev
    )
    sum_ww = lax.psum(jnp.sum(resid * resid, axis=(1, 2)), ("row", "col"))
    mean_ww = sum_ww * inverse_size
    beta_next = jnp.sqrt(mean_ww + epsilon)
    return (resid / beta_next[:, None, None], jnp.stack([coef_alpha, beta_next], axis=1))


def solution(mesh):
    placed = (
        P(None, "row", "col"),
        P(None, "row", "col"),
        P(),
        P("row"),
        P("col"),
        P(("row", "col"), None),
        P(("row", "col"), None),
        P("row", "col"),
        P("row", "col"),
    )
    return jax.shard_map(
        per_device,
        mesh=mesh,
        in_specs=placed,
        out_specs=(P(None, "row", "col"), P()),
        check_vma=False,
    )
```

profile of v0, /device:TPU:0, one launch (start us, length us, event | category | flops | bytes accessed | tf_op | source)
XLA Modules:
  0.0 517.7 jit_solution(11263954735266079760)
XLA Ops:
  7.2 3.5 all_gather.15
  10.8 57.7 %all-gather.7.cloned.1.call-done = f32[1,256,1024]{2,1,0:T(8,128)} async-done(((f32[1,16,1024]{2,1,0:T(8,128)}), f32[1,256,1024]{2,1,0:T(8,128)}) %all-gather.7.cloned.1.call-update) | async-done | bytes 1048592 | tf_op jit(solution)/shard_map/all_gather | solution.py:27
  68.6 4.5 fusion.21
  73.9 4.1 multiply_reduce_fusion
  78.0 39.9 %all-gather.2 = f32[32,1,512]{2,1,0:T(1,128)S(1)} all-gather(f32[1,1,512]{2,1,0:T(1,128)S(1)} %bitcast.62), channel_id=2, replica_groups=mesh['row'=16,'col'=2] {'row','col'}, dimensions={0}, use_global_device_ids=true | all-gather | bytes 67584 | tf_op jit(solution)/shard_map/all_gather | solution.py:33
  117.9 30.6 %convolution_bitcast_fusion.1 = f32[1024,1]{1,0:T(8,128)} fusion(f32[8192,1]{0,1:T(1,128)S(1)} %bitcast.57, f32[1024,8192]{1,0:T(8,128)} %param.17), kind=kOutput, calls=%fused_computation.15 | convolution fusion | flops 100663296 | bytes 33591296 | tf_op jit(solution)/shard_map/dot_general | solution.py:48
  148.7 51.1 %all-gather.9.cloned.1.call-done = f32[16384,256]{1,0:T(8,128)} async-done(((f32[512,256]{1,0:T(8,128)}), f32[16384,256]{1,0:T(8,128)}) %all-gather.9.cloned.1.call-update) | async-done | bytes 16777232 | tf_op jit(solution)/shard_map/all_gather | solution.py:32
  199.8 32.1 %fusion.3 = f32[1024,8192]{1,0:T(8,128)} fusion(f32[1024,256]{1,0:T(8,128)} %all-gather.11.cloned.1.call-done, f32[16384,256]{1,0:T(8,128)} %all-gather.9.cloned.1.call-done, s32[]{:T(128)S(6)} %select_n.4), kind=kOutput, calls=%fused_computation.4 | convolution fusion | flops 25769803776 | bytes 42991620 | tf_op jit(solution)/shard_map/mkv,nv->mkn/dot_general | solution.py:39
  231.9 33.1 %fusion.13 = f32[1024,1,256]{2,0,1:T(8,128)} fusion(f32[16384,256]{1,0:T(8,128)} %all-gather.9.cloned.1.call-done, s32[]{:T(128)S(6)} %select_n.4, f32[1024,8192]{1,0:T(8,128)} %fusion.3, f32[1024,8192]{1,0:T(8,128)} %param.16), kind=kOutput, calls=%fused_computation.13 | convolution fusion | flops 25778192384 | bytes 76546048 | tf_op jit(solution)/shard_map/mkn,nv->mkv/dot_general | solution.py:47
  265.3 1.1 copy.43
  266.4 5.4 %reduce-scatter.8.cloned.1.call-done = f32[512,1,256]{2,0,1:T(8,128)} async-done(((f32[1024,1,256]{2,0,1:T(8,128)}), f32[512,1,256]{2,0,1:T(8,128)}) %reduce-scatter.8.cloned.1.call-update) | async-done | bytes 524304 | tf_op jit(solution)/shard_map/reduce_scatter | solution.py:50
  271.8 4.5 convolution_bitcast_fusion
  276.3 4.6 fusion.18
  280.9 3.6 copy.36
  285.8 112.5 %all-reduce.4.cloned.1.call-done = f32[256,1,1024]{2,1,0:T(1,128)} async-done(((f32[256,1,1024]{2,1,0:T(1,128)}), f32[256,1,1024]{2,1,0:T(1,128)}) %all-reduce.4.cloned.1.call-update) | async-done | bytes 1048592
  398.3 0.8 constant_dynamic-slice_fusion
  399.2 5.9 %copy.44 = f32[16,1,1024]{1,0,2:T(8,128)} copy(f32[16,1,1024]{2,1,0:T(1,128)S(1)} %constant_dynamic-slice_fusion) | data formatting | bytes 131072
  405.0 6.5 %bitcast_reduce_fusion = f32[1024,16]{1,0:T(8,128)} fusion(f32[16,1,1024]{1,0,2:T(8,128)} %copy.44), kind=kLoop, calls=%fused_computation.2 | loop fusion | bytes 131072
  412.8 5.9 %reduce-scatter.12.cloned.1.call-done = f32[512,16]{1,0:T(8,128)} async-done(((f32[1024,16]{1,0:T(8,128)}), f32[512,16]{1,0:T(8,128)}) %reduce-scatter.12.cloned.1.call-update) | async-done | bytes 32784
  418.7 3.4 reshape_bitcast_fusion
  422.1 2.8 copy.45
  425.0 0.8 multiply_reduce_fusion.3
  425.8 40.6 %all-reduce.1 = (f32[1]{0:T(128)}, f32[1]{0:T(128)}) all-reduce(f32[1]{0:T(128)} %bitcast.15, f32[1]{0:T(128)} %bitcast.16), channel_id=1, replica_groups=mesh['row'=16,'col'=2] {'row','col'}, use_global_device_ids=true, to_apply=%region_6.0 | all-reduce | flops 2 | bytes 16 | tf_op jit(solution)/shard_map/psum | solution.py:64
  468.5 40.5 %psum.23 = f32[1]{0:T(128)} all-reduce(f32[1]{0:T(128)} %bitcast.19), channel_id=1, replica_groups=mesh['row'=16,'col'=2] {'row','col'}, use_global_device_ids=true, to_apply=%region_10.0 | all-reduce | flops 1 | bytes 8 | tf_op jit(solution)/shard_map/psum | solution.py:75
  (37 shorter events, 4.6 us)
Async XLA Ops:
  7.2 61.4 %all-gather.7.cloned.1.call-start = ((), (), s32[]{:S(2)}) async-start(), calls=%async_computation.3 | async-start | bytes 1114112 | tf_op jit(solution)/shard_map/all_gather | solution.py:27
  10.8 137.9 %all-gather.11.cloned.1.call-start = ((), (), s32[]{:S(2)}) async-start(), calls=%async_computation.6 | async-start | bytes 1572864 | tf_op jit(solution)/shard_map/all_gather | solution.py:41
  73.1 126.7 %all-gather.9.cloned.1.call-start = ((), (), s32[]{:S(2)}) async-start(), calls=%async_computation.4 | async-start | bytes 17301504 | tf_op jit(solution)/shard_map/all_gather | solution.py:32
  73.8 191.5 %reduce-scatter.10.cloned.1.call-start = ((), (), s32[]{:S(2)}) async-start(), calls=%async_computation.7 | async-start | bytes 786432
  148.5 123.3 %reduce-scatter.8.cloned.1.call-start = ((), (), s32[]{:S(2)}) async-start(), calls=%async_computation.5 | async-start | bytes 1572864 | tf_op jit(solution)/shard_map/reduce_scatter | solution.py:50
  231.9 39.9 %copy-start = (f32[512,1024]{1,0:T(8,128)S(1)}, f32[512,1024]{1,0:T(8,128)}, u32[]{:S(2)}) copy-start(f32[512,1024]{1,0:T(8,128)} %param.15) | copy-start | bytes 6291460
  231.9 44.4 %copy-start.1 = (f32[512,256]{1,0:T(8,128)S(1)}, f32[512,256]{1,0:T(8,128)}, u32[]{:S(2)}) copy-start(f32[512,256]{1,0:T(8,128)} %param.14) | copy-start | bytes 1572868
  265.0 19.6 %copy-start.6 = (u32[32]{0:T(128)S(1)}, u32[32]{0:T(128)}, u32[]{:S(2)}) copy-start(u32[32]{0:T(128)} %constant.20) | copy-start | bytes 388
  265.0 133.3 %all-reduce.4.cloned.1.call-start = ((), (), s32[]{:S(2)}) async-start(), calls=%async_computation.9 | async-start | bytes 2097152
  284.5 134.2 %reduce-scatter.12.cloned.1.call-start = ((), (), s32[]{:S(2)}) async-start(), calls=%async_computation.8 | async-start | bytes 786432
  399.2 13.0 %copy-start.2 = (f32[1,16,512]{2,1,0:T(8,128)S(1)}, f32[1,16,512]{2,1,0:T(8,128)}, u32[]{:S(2)}) copy-start(f32[1,16,512]{2,1,0:T(8,128)} %param.9) | copy-start | bytes 98308
  405.0 20.0 %copy-start.4 = (f32[512]{0:T(512)S(1)}, f32[512]{0:T(512)}, u32[]{:S(2)}) copy-start(f32[512]{0:T(512)} %param.13) | copy-start | bytes 6148
  405.0 20.0 %copy-start.5 = (f32[16]{0:T(128)S(1)}, f32[16]{0:T(128)}, u32[]{:S(2)}) copy-start(f32[16]{0:T(128)} %param.12) | copy-start | bytes 196
  405.0 62.8 %copy-start.3 = (f32[1,16,512]{2,1,0:T(8,128)S(1)}, f32[1,16,512]{2,1,0:T(8,128)}, u32[]{:S(2)}) copy-start(f32[1,16,512]{2,1,0:T(8,128)} %param.10) | copy-start | bytes 98308
Sparse Core Ops, SparseCore 0:
  10.9 57.6 all-gather.6
  73.2 7.8 all-gather.10
  84.0 115.7 all-gather.8
  201.9 6.1 reduce-scatter.9
  265.1 6.5 reduce-scatter.7
  284.6 113.6 all-reduce.3
  411.7 6.9 reduce-scatter.11
where the time goes:
time: 518 us
  waiting for transfers between devices  233 us (45%)
  blocking collectives  125 us (24%)
  matrix products  113 us (22%)
  local copies, waits for them, and re-layouts  25.4 us (5%)
  between operations  17.6 us (3%)
    unnamed x10, waiting for transfers between devices  119 us
    all_gather x1, waiting for transfers between devices, per_device(): vectors = lax.all_gather(wider, 'row', axis=1, tiled=True)  57.7 us
    all_gather x1, waiting for transfers between devices, per_device(): lax.all_gather(valence_panel, ('row', 'col'), axis=0, tiled=True)  51.1 us
    psum x1, blocking collectives, per_device(): lax.psum((jnp.sum(lanczos_now * image, axis=(1, 2)), jnp.sum(lanczos_now...  40.6 us
    psum x1, blocking collectives, per_device(): sum_ww = lax.psum(jnp.sum(resid * resid, axis=(1, 2)), ('row', 'col'))  40.5 us
    all_gather x1, blocking collectives, per_device(): lax.all_gather(density, ('row', 'col'), axis=0, tiled=True)  39.9 us
    dot_general x1, matrix products, per_device(): screened = jnp.einsum('mkn,nv->mkv', pair_terms, panel, precision=precise)  33.1 us
    dot_general x1, matrix products, per_device(): jnp.einsum('mkv,nv->mkn', lax.all_gather(pair_local, 'col', axis=0, tiled...  32.1 us
  transfers between devices with their start and end apart: 7, of which 5 were waited for; matrix products, arithmetic and copies ran while one was open for 20% of the time, Pallas kernels for 0%

commit v1 on v0

v1 whole, which is shorter than its diff:
```python
import functools

import jax
import jax.numpy as jnp
from jax import lax
from jax.experimental import pallas as pl
from jax.experimental.pallas import tpu as pltpu
from jax.sharding import PartitionSpec as P

MESH = pl.DeviceIdType.MESH
F32 = jnp.float32
BF16 = jnp.bfloat16
epsilon = 1e-06
LANES = 128
EXTRA = 8


def split(a):
    high = a.astype(BF16)
    return high, (a - high.astype(F32)).astype(BF16)


def dot3(a, b, dims):
    (ah, al), (bh, bl) = a, b
    one = functools.partial(lax.dot_general, dimension_numbers=(dims, ((), ())), preferred_element_type=F32)
    return one(ah, bh) + (one(ah, bl) + one(al, bh))


def flip(index, mask):
    bit = 0
    while mask >> bit:
        if (mask >> bit) & 1:
            index = index + (1 - 2 * ((index // (1 << bit)) % 2)) * (1 << bit)
        bit += 1
    return index


def remote(src, dst, send, recv, where):
    return pltpu.make_async_remote_copy(
        src_ref=src, dst_ref=dst, send_sem=send, recv_sem=recv, device_id=where, device_id_type=MESH
    )


def loop(low, high, body):
    def step(k, carry):
        body(k)
        return carry

    lax.fori_loop(low, high, step, 0)


def vectors_kernel(nrow, ncol, x_ref, full_ref, local_sem, rs, rr, cs, cr):
    r, c = lax.axis_index("row"), lax.axis_index("col")
    h, w = x_ref.shape

    def row_copy(k):
        return remote(
            x_ref, full_ref.at[c, pl.ds(r * h, h)], rs.at[k], rr.at[k], (lax.rem(r + k, nrow), c)
        )

    def col_copy(k):
        return remote(full_ref.at[c], full_ref.at[c], cs.at[k], cr.at[k], (r, lax.rem(c + k, ncol)))

    def col_arrival(k):
        there = lax.rem(c + ncol - k, ncol)
        return remote(full_ref.at[there], full_ref.at[there], cs.at[k], cr.at[k], (r, there))

    def row_arrival(k):
        there = lax.rem(r + nrow - k, nrow)
        part = full_ref.at[c, pl.ds(there * h, h)]
        return remote(x_ref, part, rs.at[k], rr.at[k], (there, c))

    loop(1, nrow, lambda k: row_copy(k).start())
    own = pltpu.make_async_copy(x_ref, full_ref.at[c, pl.ds(r * h, h)], local_sem)
    own.start()
    own.wait()
    loop(1, nrow, lambda k: row_arrival(k).wait_recv())
    loop(1, ncol, lambda k: col_copy(k).start())
    loop(1, ncol, lambda k: col_arrival(k).wait_recv())
    loop(1, nrow, lambda k: row_copy(k).wait_send())
    loop(1, ncol, lambda k: col_copy(k).wait_send())


def kernel_kernel(
    nrow, ncol, blk, item_ref, pair_ref, w_ref, b_ref, s_ref,
    pan, pairs, ah, al, ph, plo, wbuf, bbuf,
    wsem, bsem, local_sem, chip_send, top_send, send, recv, pair_send, pair_recv,
):
    r, c = lax.axis_index("row"), lax.axis_index("col")
    per = nrow // ncol
    bits = per.bit_length() - 1
    tops = ncol.bit_length() - 1
    top, low = r // per, lax.rem(r, per)
    bands = pair_ref.shape[1]
    points = ncol * blk
    unit = wbuf.shape[3] // blk
    units = ncol // unit
    if bits >= 2:
        base = list(range(bits - 1, 1, -1))
        orders = (base + [0, 1], base + [1, 0])
    else:
        orders = (list(range(bits)),) * 2
    positions = sorted(range(per), key=lambda p: (bin(p).count("1"), p))

    def mask_of(i, position):
        return sum(1 << b for at, b in enumerate(orders[(i // unit) % 2]) if (position >> at) & 1)

    def slot(i, mask):
        return flip(low, mask) * ncol + i

    def fetch(u, step, buffer):
        near = slot(u * unit, mask_of(u * unit, positions[step]))
        at = pl.ds(pl.multiple_of(near * blk, unit * blk), unit * blk)
        return (
            pltpu.make_async_copy(w_ref.at[:, at], wbuf.at[buffer, u], wsem.at[buffer, u]),
            pltpu.make_async_copy(b_ref.at[:, at], bbuf.at[buffer, u], bsem.at[buffer, u]),
        )

    def start_fetch(step):
        for u in range(units):
            for copy in fetch(u, step, step % 2):
                copy.start()

    for j in range(ncol):
        mine = c == j
        here = pan.at[low * ncol + j]

        @pl.when(jnp.logical_and(mine, top == c))
        def _():
            pltpu.make_async_copy(item_ref, here, local_sem).start()

        @pl.when(jnp.logical_and(mine, top != c))
        def _():
            remote(item_ref, here, chip_send, recv.at[j, 0], (r, top)).start()

    def pair_copy(k):
        return remote(
            pair_ref, pairs.at[c], pair_send.at[k], pair_recv.at[k], (r, lax.rem(c + k, ncol))
        )

    def pair_arrival(k):
        there = lax.rem(c + ncol - k, ncol)
        return remote(pair_ref, pairs.at[there], pair_send.at[k], pair_recv.at[k], (r, there))

    loop(1, ncol, lambda k: pair_copy(k).start())
    start_fetch(0)
    if per > 1:
        start_fetch(1)
    s_ref[...] = jnp.zeros_like(s_ref)
    pairs[c] = pair_ref[...]

    def top_copy(i, bit):
        here = pan.at[low * ncol + i]
        return remote(
            here, here, top_send.at[i, bit], recv.at[i, 0], (flip(top, 1 << bit) * per + low, c)
        )

    def differs(bit):
        return lax.rem(top, 2 << bit) == lax.rem(c, 2 << bit)

    def forward_copy(i, mask, stage):
        b = orders[(i // unit) % 2][stage]
        part = pan.at[slot(i, mask)]
        return remote(
            part, part, send.at[i, mask, stage], recv.at[i, mask ^ (1 << b)],
            (flip(r, 1 << b), c),
        )

    def arrival(i, mask):
        part = pan.at[slot(i, mask)]
        return remote(part, part, chip_send, recv.at[i, mask], (r, c))

    def stages(position):
        return range(position.bit_length(), bits)

    for step, position in enumerate(positions):
        for i in range(ncol):
            mask = mask_of(i, position)
            if position == 0:

                @pl.when(jnp.logical_and(c == i, top == c))
                def _():
                    pltpu.make_async_copy(item_ref, pan.at[low * ncol + i], local_sem).wait()

                @pl.when(jnp.logical_not(jnp.logical_and(c == i, top == c)))
                def _():
                    arrival(i, 0).wait_recv()

                for bit in reversed(range(tops)):

                    @pl.when(differs(bit))
                    def _():
                        top_copy(i, bit).start()
            else:
                arrival(i, mask).wait_recv()
            for stage in stages(position):
                forward_copy(i, mask, stage).start()
        if position == 0:
            loop(1, ncol, lambda k: pair_arrival(k).wait_recv())
            for j in range(ncol):
                high, rest = split(pairs[j])
                ah[j * blk : (j + 1) * blk] = high
                al[j * blk : (j + 1) * blk] = rest
        buffer = step % 2
        for i in range(ncol):
            high, rest = split(pan[slot(i, mask_of(i, position)), :blk])
            at = slice((i % unit) * blk, (i % unit + 1) * blk)
            ph[i // unit, at] = high
            plo[i // unit, at] = rest
        for u in range(units):
            for copy in fetch(u, step, buffer):
                copy.wait()
        rows = min(256, points)
        width = min(blk, bands)

        for u in range(units):
            p2 = (ph[u], plo[u])
            lines = [
                pan[slot(i, mask_of(i, position)), blk : blk + EXTRA][j : j + 1, :width]
                for i in range(u * unit, (u + 1) * unit)
                for j in range(blk // width)
            ]

            def body(m):
                at = pl.ds(pl.multiple_of(m * rows, rows), rows)
                terms = dot3((ah[at], al[at]), p2, ((1,), (1,))) * wbuf[buffer, u, at]
                s_ref[at, :bands] += dot3(split(terms), p2, ((1,), (0,)))
                total = jnp.zeros((rows, 1), F32)
                for j, line in enumerate(lines):
                    part = bbuf[buffer, u, at, j * width : (j + 1) * width] * line
                    total = total + jnp.sum(part, axis=1, keepdims=True)
                s_ref[at, bands:] += jnp.broadcast_to(total, (rows, LANES))

            loop(0, points // rows, body)
        if step + 2 < per:
            start_fetch(step + 2)

    loop(1, ncol, lambda k: pair_copy(k).wait_send())

    @pl.when(top != c)
    def _():
        remote(item_ref, pan.at[low * ncol], chip_send, recv.at[0, 0], (r, top)).wait_send()

    for i in range(ncol):
        for bit in range(tops):

            @pl.when(differs(bit))
            def _():
                top_copy(i, bit).wait_send()

        for position in positions:
            for stage in stages(position):
                forward_copy(i, mask_of(i, position), stage).wait_send()


def last_kernel(
    nrow, ncol, size, s_ref, pv_ref, pc_ref, x_ref, prev_ref, gap_ref, beta_ref, out_ref, coef_ref,
    sin, kbuf, kin, rbuf, rin, tile1, tin1, tile2, tin2,
    s_send, s_recv, k_send, k_recv, r_send, r_recv, t1_send, t1_recv, t2_send, t2_recv,
):
    r, c = lax.axis_index("row"), lax.axis_index("col")
    blk, bands = pv_ref.shape
    h, w = x_ref.shape
    everyone = nrow * ncol
    me = r * ncol + c

    def col_peer(k):
        return lax.rem(c + k, ncol)

    def row_peer(k):
        return lax.rem(r + k, nrow)

    def s_copy(k):
        at = pl.ds(pl.multiple_of(col_peer(k) * blk, blk), blk)
        return remote(s_ref.at[at], sin.at[k], s_send.at[k], s_recv.at[k], (r, col_peer(k)))

    def k_copy(k):
        return remote(kbuf.at[col_peer(k)], kin.at[k], k_send.at[k], k_recv.at[k], (r, col_peer(k)))

    def r_copy(k):
        return remote(rbuf.at[row_peer(k)], rin.at[k], r_send.at[k], r_recv.at[k], (row_peer(k), c))

    loop(1, ncol, lambda k: s_copy(k).start())
    own = s_ref[pl.ds(pl.multiple_of(c * blk, blk), blk)]
    for k in range(1, ncol):
        s_copy(k).wait_recv()
        own = own + sin[k]
    terms = 2.0 * pv_ref[...] * own[:, bands : bands + 1] - own[:, :bands]
    turned = split(jnp.transpose(terms))
    for j in range(ncol):
        kbuf[j] = dot3(turned, split(pc_ref[:, j * w : (j + 1) * w]), ((1,), (0,)))
    loop(1, ncol, lambda k: k_copy(k).start())
    part = kbuf[c]
    for k in range(1, ncol):
        k_copy(k).wait_recv()
        part = part + kin[k]
    rbuf[...] = part.reshape(nrow, h, w)
    loop(1, nrow, lambda k: r_copy(k).start())
    x = x_ref[...]
    image = gap_ref[...] * x + rbuf[r]
    for k in range(1, nrow):
        r_copy(k).wait_recv()
        image = image + rin[k]

    def whole(a):
        return jnp.sum(jnp.sum(a, axis=0, keepdims=True), axis=1, keepdims=True)

    def shared(value, tile, tin, sends, recvs):
        def copy(k):
            there = lax.rem(me + k, everyone)
            return remote(tile, tin.at[me], sends.at[k], recvs.at[k], (there // ncol, lax.rem(there, ncol)))

        def arrival(k):
            there = lax.rem(me + everyone - k, everyone)
            return remote(tile, tin.at[there], sends.at[k], recvs.at[k], (there // ncol, lax.rem(there, ncol)))

        tile[...] = value
        tin[me] = value
        loop(1, everyone, lambda k: copy(k).start())
        loop(1, everyone, lambda k: arrival(k).wait_recv())
        loop(1, everyone, lambda k: copy(k).wait_send())
        return jnp.sum(tin[...], axis=0)

    line = lax.broadcasted_iota(jnp.int32, (8, LANES), 0)
    sums = shared(jnp.where(line == 0, whole(x * image), whole(x * x)), tile1, tin1, t1_send, t1_recv)
    alpha = (sums[0:1, 0:1] / size) / (sums[1:2, 0:1] / size + epsilon)
    resid = image - alpha * x - beta_ref[...] * prev_ref[...]
    square = jnp.broadcast_to(whole(resid * resid), (8, LANES))
    beta = jnp.sqrt(shared(square, tile2, tin2, t2_send, t2_recv)[0:1, 0:1] / size + epsilon)
    out_ref[...] = resid / beta
    coef_ref[...] = jnp.where(line == 0, alpha, beta)
    loop(1, ncol, lambda k: s_copy(k).wait_send())
    loop(1, ncol, lambda k: k_copy(k).wait_send())
    loop(1, nrow, lambda k: r_copy(k).wait_send())


VM = pl.BlockSpec(memory_space=pltpu.VMEM)
DMA = pltpu.SemaphoreType.DMA
PARAMS = pltpu.CompilerParams(has_side_effects=True, vmem_limit_bytes=56 * 1024 * 1024)


def per_device(
    nrow, ncol, lanczos_now, lanczos_prev, beta_prev, valence_energy, conduction_energy,
    valence_panel, conduction_panel, screened_coulomb, bare_coulomb,
):
    chains, h, w = lanczos_now.shape
    blk, bands = valence_panel.shape
    conduction = conduction_panel.shape[1]
    points = screened_coulomb.shape[0]
    outs = []
    for chain in range(chains):
        x = lanczos_now[chain]
        full = pl.pallas_call(
            functools.partial(vectors_kernel, nrow, ncol),
            out_shape=jax.ShapeDtypeStruct((ncol, bands, w), F32),
            in_specs=[VM],
            out_specs=VM,
            scratch_shapes=[DMA(()), DMA((nrow,)), DMA((nrow,)), DMA((ncol,)), DMA((ncol,))],
            compiler_params=PARAMS,
        )(x)
        vectors = jnp.transpose(full, (1, 0, 2)).reshape(bands, conduction)
        pair = lax.dot_general(
            conduction_panel, vectors, (((1,), (1,)), ((), ())), precision=lax.Precision.HIGH,
            preferred_element_type=F32,
        )
        density = jnp.sum(pair * valence_panel, axis=1)
        width = min(blk, bands)
        lines = density.reshape(blk // width, width)
        lines = jnp.pad(lines, ((0, EXTRA - blk // width), (0, bands - width)))
        item = jnp.concatenate([valence_panel, lines], axis=0)
        unit = max(1, LANES // blk)
        per = nrow // ncol
        stages = max(1, per.bit_length() - 1)
        tops = max(1, ncol.bit_length() - 1)
        screened = pl.pallas_call(
            functools.partial(kernel_kernel, nrow, ncol, blk),
            out_shape=jax.ShapeDtypeStruct((points, bands + LANES), F32),
            in_specs=[VM, VM, pl.BlockSpec(memory_space=pl.ANY), pl.BlockSpec(memory_space=pl.ANY)],
            out_specs=VM,
            scratch_shapes=[
                pltpu.VMEM((nrow, blk + EXTRA, bands), F32),
                pltpu.VMEM((ncol, blk, bands), F32),
                pltpu.VMEM((points, bands), BF16),
                pltpu.VMEM((points, bands), BF16),
                pltpu.VMEM((ncol // unit, unit * blk, bands), BF16),
                pltpu.VMEM((ncol // unit, unit * blk, bands), BF16),
                pltpu.VMEM((2, ncol // unit, points, unit * blk), F32),
                pltpu.VMEM((2, ncol // unit, points, unit * blk), F32),
                DMA((2, ncol)),
                DMA((2, ncol)),
                DMA(()),
                DMA(()),
                DMA((ncol, tops)),
                DMA((ncol, per, stages)),
                DMA((ncol, per)),
                DMA((ncol,)),
                DMA((ncol,)),
            ],
            compiler_params=PARAMS,
        )(item, pair, screened_coulomb, bare_coulomb)
        gaps = conduction_energy[None, :] - valence_energy[:, None]
        beta = jnp.broadcast_to(beta_prev[chain], (1, w))
        everyone = nrow * ncol
        out, coef = pl.pallas_call(
            functools.partial(last_kernel, nrow, ncol, float(bands * conduction)),
            out_shape=(jax.ShapeDtypeStruct((h, w), F32), jax.ShapeDtypeStruct((8, LANES), F32)),
            in_specs=[VM] * 7,
            out_specs=(VM, VM),
            scratch_shapes=[
                pltpu.VMEM((ncol, blk, bands + LANES), F32),
                pltpu.VMEM((ncol, bands, w), F32),
                pltpu.VMEM((ncol, bands, w), F32),
                pltpu.VMEM((nrow, h, w), F32),
                pltpu.VMEM((nrow, h, w), F32),
                pltpu.VMEM((8, LANES), F32),
                pltpu.VMEM((everyone, 8, LANES), F32),
                pltpu.VMEM((8, LANES), F32),
                pltpu.VMEM((everyone, 8, LANES), F32),
            ]
            + [DMA((n,)) for n in (ncol, ncol, ncol, ncol, nrow, nrow) for _ in range(1)]
            + [DMA((everyone,))] * 4,
            compiler_params=PARAMS,
        )(screened, valence_panel, conduction_panel, x, lanczos_prev[chain], gaps, beta)
        outs.append((out, coef[:2, 0]))
    return jnp.stack([o for o, _ in outs]), jnp.stack([k for _, k in outs])


def solution(mesh):
    placed = (
        P(None, "row", "col"),
        P(None, "row", "col"),
        P(),
        P("row"),
        P("col"),
        P(("row", "col"), None),
        P(("row", "col"), None),
        P("row", "col"),
        P("row", "col"),
    )
    return jax.shard_map(
        functools.partial(per_device, mesh.shape["row"], mesh.shape["col"]),
        mesh=mesh,
        in_specs=placed,
        out_specs=(P(None, "row", "col"), P()),
        check_vma=False,
    )
```

time: 518 us -> 181 us (0.35)
  waiting for transfers between devices: 233 us -> 0 us
  Pallas kernels: 0 us -> 168 us
  blocking collectives: 125 us -> 0 us
  matrix products: 113 us -> 2.39 us
  local copies, waits for them, and re-layouts: 25.4 us -> 7.86 us
  between operations: 17.6 us -> 1.35 us
    pallas_call x0 -> x3, Pallas kernels: none -> 168 us  [the longest x1 96.3 us: per_device(): pl.pallas_call(functools.partial(kernel_kernel, nrow, ncol, blk), out_sha...]
    unnamed x10 -> x0, waiting for transfers between devices: 119 us -> none
    dot_general x7 -> x1, matrix products: 113 us -> 2.39 us  [per_device(): lax.dot_general(conduction_panel, vectors, (((1,), (1,)), ((), ())), prec...]
    all_gather x3 -> x0, waiting for transfers between devices: 109 us -> none  [the longest x1 57.7 us: per_device(): vectors = lax.all_gather(wider, 'row', axis=1, tiled=True)]
    psum x2 -> x0, blocking collectives: 81.1 us -> none  [the longest x1 40.6 us: per_device(): lax.psum((jnp.sum(lanczos_now * image, axis=(1, 2)), jnp.sum(lanczos_now...]
    all_gather x2 -> x0, blocking collectives: 43.5 us -> none  [the longest x1 39.9 us: per_device(): lax.all_gather(density, ('row', 'col'), axis=0, tiled=True)]
    unnamed x22 -> x10, local copies, waits for them, and re-layouts: 21.8 us -> 2.41 us
    reduce_scatter x1 -> x0, waiting for transfers between devices: 5.4 us -> none  [per_device(): lax.psum_scatter(screened, 'col', scatter_dimension=0, tiled=True)]
  transfers between devices with their start and end apart: 7 -> 0, of which waited for: 5 -> 0; matrix products, arithmetic and copies ran while one was open for 20% -> 0% of each run, Pallas kernels for 0% -> 0%
where the time goes in v1:
time: 181 us
  Pallas kernels  168 us (93%)
  local copies, waits for them, and re-layouts  7.86 us (4%)
  matrix products  2.39 us (1%)
    pallas_call x1, Pallas kernels, per_device(): pl.pallas_call(functools.partial(kernel_kernel, nrow, ncol, blk), out_sha...  96.3 us
    pallas_call x1, Pallas kernels, per_device(): pl.pallas_call(functools.partial(last_kernel, nrow, ncol, float(bands * c...  48.5 us
    pallas_call x1, Pallas kernels, per_device(): pl.pallas_call(functools.partial(vectors_kernel, nrow, ncol), out_shape=j...  23 us

profile of v1, /device:TPU:0, one launch (start us, length us, event | category | flops | bytes accessed | tf_op | source)
XLA Modules:
  0.0 181.0 jit_solution(18080963978278485958)
XLA Ops:
  0.6 0.0 copy-start.1
  0.6 0.0 copy-start
  0.7 23.0 %shard_map.104 = f32[2,256,512]{2,1,0:T(8,128)} custom-call(f32[16,512]{1,0:T(8,128)} %bitcast.12), custom_call_target="tpu_custom_call" | custom-call | tf_op jit(solution)/shard_map/pallas_call | solution.py:353
  23.7 2.5 %copy.13 = f32[256,2,512]{0,2,1:T(8,128)} copy(f32[256,2,512]{2,0,1:T(8,128)} %bitcast.10) | data formatting | bytes 2097152 | tf_op jit(solution)/shard_map/transpose | solution.py:361
  26.2 0.0 copy-done.1
  26.2 1.0 copy.14
  27.2 0.0 copy-done
  27.2 2.4 %multiply_reduce_fusion = (f32[512]{0:T(512)S(1)}, f32[512,256]{0,1:T(8,128)S(1)}) fusion(f32[512,256]{0,1:T(8,128)} %copy.14, f32[512,1024]{1,0:T(8,128)S(1)} %copy-done, f32[256,1024]{0,1:T(8,128)} %bitcast.11), kind=kOutput, calls=%fused_computation.2 | convolution fusion | flops 805568000 | bytes 4196352 | tf_op jit(solution)/shard_map/dot_general | solution.py:362
  29.6 0.8 select_maximum_fusion.item_ref
  30.5 1.0 copy.15.pair_ref
  31.5 0.0 copy-start.2
  31.5 0.0 copy-start.3
  31.5 96.3 %shard_map.105.s_ref = f32[1024,384]{1,0:T(8,128)} custom-call(f32[520,256]{1,0:T(8,128)} %select_maximum_fusion.item_ref, f32[512,256]{1,0:T(8,128)} %copy.15.pair_ref, f32[1024,8192]{1,0:T(8,128)} %w_ref.1, f32[1024,8192]{1,0:T(8,128)} %b_ref.1), custom_call_target="tpu_custom_call" | custom-call | tf_op jit(solution)/shard_map/pallas_call | solution.py:375
  127.8 0.0 copy-done.2
  127.8 0.0 copy-done.3
  127.8 0.7 broadcast_subtract_fusion.gap_ref
  129.2 0.6 broadcast_in_dim.2.beta_ref
  129.8 48.5 %shard_map.106 = (f32[16,512]{1,0:T(8,128)}, f32[8,128]{1,0:T(8,128)}) custom-call(f32[1024,384]{1,0:T(8,128)} %shard_map.105.s_ref, f32[512,256]{1,0:T(8,128)} %pv_ref.1, f32[512,1024]{1,0:T(8,128)} %pc_ref.1, f32[16,512]{1,0:T(8,128)} %bitcast.13, f32[16,512]{1,0:T(8,128)} %bitcast.14, f32[16,512]{1,0:T(8,128)} %broadcast_subtract_fusion.gap_ref, ...), custom_call_target="tpu_custom_call" | custom-call | tf_op jit(solution)/shard_map/pallas_call | solution.py:404
  178.3 1.3 slice_reduce_fusion
  179.6 1.4 copy.18
  (1 shorter events, 0.0 us)
Async XLA Ops:
  0.6 25.6 %copy-start.1 = (f32[512,256]{1,0:T(8,128)S(1)}, f32[512,256]{1,0:T(8,128)}, u32[]{:S(2)}) copy-start(f32[512,256]{1,0:T(8,128)} %pv_ref.1) | copy-start | bytes 1572868
  0.6 26.6 %copy-start = (f32[512,1024]{1,0:T(8,128)S(1)}, f32[512,1024]{1,0:T(8,128)}, u32[]{:S(2)}) copy-start(f32[512,1024]{1,0:T(8,128)} %pc_ref.1) | copy-start | bytes 6291460
  31.5 96.3 %copy-start.2 = (f32[512]{0:T(512)S(1)}, f32[512]{0:T(512)}, u32[]{:S(2)}) copy-start(f32[512]{0:T(512)} %param.13) | copy-start | bytes 6148
  31.5 96.3 %copy-start.3 = (f32[16]{0:T(128)S(1)}, f32[16]{0:T(128)}, u32[]{:S(2)}) copy-start(f32[16]{0:T(128)} %param.12) | copy-start | bytes 196

commit v2 on v1

--- a/solution.py
+++ b/solution.py
@@ -322,10 +322,11 @@
         return jnp.sum(tin[...], axis=0)
 
     line = lax.broadcasted_iota(jnp.int32, (8, LANES), 0)
-    sums = shared(jnp.where(line == 0, whole(x * image), whole(x * x)), tile1, tin1, t1_send, t1_recv)
-    alpha = (sums[0:1, 0:1] / size) / (sums[1:2, 0:1] / size + epsilon)
+    lane = lax.broadcasted_iota(jnp.int32, (1, LANES), 1)
+    sums = shared(jnp.where(lane == 0, whole(x * image), whole(x * x)), tile1, tin1, t1_send, t1_recv)
+    alpha = (sums[0:1, 0:1] / size) / (sums[0:1, 1:2] / size + epsilon)
     resid = image - alpha * x - beta_ref[...] * prev_ref[...]
-    square = jnp.broadcast_to(whole(resid * resid), (8, LANES))
+    square = jnp.broadcast_to(whole(resid * resid), (1, LANES))
     beta = jnp.sqrt(shared(square, tile2, tin2, t2_send, t2_recv)[0:1, 0:1] / size + epsilon)
     out_ref[...] = resid / beta
     coef_ref[...] = jnp.where(line == 0, alpha, beta)
@@ -412,10 +413,10 @@
                 pltpu.VMEM((ncol, bands, w), F32),
                 pltpu.VMEM((nrow, h, w), F32),
                 pltpu.VMEM((nrow, h, w), F32),
-                pltpu.VMEM((8, LANES), F32),
-                pltpu.VMEM((everyone, 8, LANES), F32),
-                pltpu.VMEM((8, LANES), F32),
-                pltpu.VMEM((everyone, 8, LANES), F32),
+                pltpu.VMEM((1, LANES), F32),
+                pltpu.VMEM((everyone, 1, LANES), F32),
+                pltpu.VMEM((1, LANES), F32),
+                pltpu.VMEM((everyone, 1, LANES), F32),
             ]
             + [DMA((n,)) for n in (ncol, ncol, ncol, ncol, nrow, nrow) for _ in range(1)]
             + [DMA((everyone,))] * 4,

time: 181 us -> 180 us (level)
  no operation moved by 1% of the time
where the time goes in v2:
time: 180 us
  Pallas kernels  167 us (93%)
  local copies, waits for them, and re-layouts  7.86 us (4%)
  matrix products  2.39 us (1%)
    pallas_call x1, Pallas kernels, per_device(): pl.pallas_call(functools.partial(kernel_kernel, nrow, ncol, blk), out_sha...  96.3 us
    pallas_call x1, Pallas kernels, per_device(): pl.pallas_call(functools.partial(last_kernel, nrow, ncol, float(bands * c...  47.4 us
    pallas_call x1, Pallas kernels, per_device(): pl.pallas_call(functools.partial(vectors_kernel, nrow, ncol), out_shape=j...  23 us

profile of v2, /device:TPU:0, one launch (start us, length us, event | category | flops | bytes accessed | tf_op | source)
XLA Modules:
  0.0 179.8 jit_solution(14578243464762072252)
XLA Ops:
  0.6 0.0 copy-start.1
  0.6 0.0 copy-start
  0.7 23.0 %shard_map.104 = f32[2,256,512]{2,1,0:T(8,128)} custom-call(f32[16,512]{1,0:T(8,128)} %bitcast.12), custom_call_target="tpu_custom_call" | custom-call | tf_op jit(solution)/shard_map/pallas_call | solution.py:354
  23.7 2.5 %copy.13 = f32[256,2,512]{0,2,1:T(8,128)} copy(f32[256,2,512]{2,0,1:T(8,128)} %bitcast.10) | data formatting | bytes 2097152 | tf_op jit(solution)/shard_map/transpose | solution.py:362
  26.2 0.0 copy-done.1
  26.2 1.0 copy.14
  27.2 0.0 copy-done
  27.2 2.4 %multiply_reduce_fusion = (f32[512]{0:T(512)S(1)}, f32[512,256]{0,1:T(8,128)S(1)}) fusion(f32[512,256]{0,1:T(8,128)} %copy.14, f32[512,1024]{1,0:T(8,128)S(1)} %copy-done, f32[256,1024]{0,1:T(8,128)} %bitcast.11), kind=kOutput, calls=%fused_computation.2 | convolution fusion | flops 805568000 | bytes 4196352 | tf_op jit(solution)/shard_map/dot_general | solution.py:363
  29.6 0.8 select_maximum_fusion.item_ref
  30.5 1.0 copy.15.pair_ref
  31.5 0.0 copy-start.2
  31.5 0.0 copy-start.3
  31.5 96.3 %shard_map.105.s_ref = f32[1024,384]{1,0:T(8,128)} custom-call(f32[520,256]{1,0:T(8,128)} %select_maximum_fusion.item_ref, f32[512,256]{1,0:T(8,128)} %copy.15.pair_ref, f32[1024,8192]{1,0:T(8,128)} %w_ref.1, f32[1024,8192]{1,0:T(8,128)} %b_ref.1), custom_call_target="tpu_custom_call" | custom-call | tf_op jit(solution)/shard_map/pallas_call | solution.py:376
  127.8 0.0 copy-done.2
  127.8 0.0 copy-done.3
  127.8 0.7 broadcast_subtract_fusion.gap_ref
  129.2 0.6 broadcast_in_dim.2.beta_ref
  129.8 47.4 %shard_map.106 = (f32[16,512]{1,0:T(8,128)}, f32[8,128]{1,0:T(8,128)}) custom-call(f32[1024,384]{1,0:T(8,128)} %shard_map.105.s_ref, f32[512,256]{1,0:T(8,128)} %pv_ref.1, f32[512,1024]{1,0:T(8,128)} %pc_ref.1, f32[16,512]{1,0:T(8,128)} %bitcast.13, f32[16,512]{1,0:T(8,128)} %bitcast.14, f32[16,512]{1,0:T(8,128)} %broadcast_subtract_fusion.gap_ref, ...), custom_call_target="tpu_custom_call" | custom-call | tf_op jit(solution)/shard_map/pallas_call | solution.py:405
  177.1 1.3 slice_reduce_fusion
  178.5 1.4 copy.18
  (1 shorter events, 0.0 us)
Async XLA Ops:
  0.6 25.6 %copy-start.1 = (f32[512,256]{1,0:T(8,128)S(1)}, f32[512,256]{1,0:T(8,128)}, u32[]{:S(2)}) copy-start(f32[512,256]{1,0:T(8,128)} %pv_ref.1) | copy-start | bytes 1572868
  0.6 26.6 %copy-start = (f32[512,1024]{1,0:T(8,128)S(1)}, f32[512,1024]{1,0:T(8,128)}, u32[]{:S(2)}) copy-start(f32[512,1024]{1,0:T(8,128)} %pc_ref.1) | copy-start | bytes 6291460
  31.5 96.3 %copy-start.2 = (f32[512]{0:T(512)S(1)}, f32[512]{0:T(512)}, u32[]{:S(2)}) copy-start(f32[512]{0:T(512)} %param.13) | copy-start | bytes 6148
  31.5 96.3 %copy-start.3 = (f32[16]{0:T(128)S(1)}, f32[16]{0:T(128)}, u32[]{:S(2)}) copy-start(f32[16]{0:T(128)} %param.12) | copy-start | bytes 196
